TPU v7x, 32 devices: a whole 2x2x4 slice. The times are simulated.
32 devices in a mesh: row: 8 (over y, x, core), col: 4 (over z).
Axes of the slice: x: 2, y: 2, z: 4, core: 2. Of those that a mesh axis runs over, the one named last changes fastest.
Arguments:
- singular_vectors: float32 [4096, 4096], P('row', 'col'), may hold values from -6 to 6
- reflector_vectors: float32 [2, 16, 256, 512], P(None, 'row', 'col'), may hold values from -2 to 2, as said below
- reflector_factors: float32 [2, 16, 256, 256], P(None, 'row', 'col'), as said below
- sweep_bounds: int32 [2, 2], replicated, may hold values from 0 to 3584, as said below
Outputs:
- transformed: float32 [4096, 4096], P('row', 'col')
Inputs may be any that keep to these rules, and one draw needn't show every extreme that they name: `reflector_vectors`: row j of each block's 256 x 2 * 256 slice is a reflector: 1 at position j, nonzero only at positions j to j + 255. `reflector_factors`: each block's factor is the upper triangular inverse of the strictly upper part of W W^T plus half of its diagonal, W being that block's slice of reflector_vectors, so that each block's transformation is orthogonal. `sweep_bounds`: both entries are multiples of 256, and the first is below the second.
All inputs are finite; a program needn't handle non-finite values.
Results may differ from a plain program's by a relative error of at most 0.0003.
Values sent between devices are 32-bit elements; how exact they have to be, the bound alone decides.
A program may use at most 64 MiB of HBM per device.

v0:
```python
import jax
import jax.numpy as jnp
from jax import lax
from jax.sharding import PartitionSpec as P

exact_mode = lax.Precision.HIGHEST


def extended_2(block, sides, width):
    for axis, dim in sides:
        count = lax.axis_size(axis)
        forward = [(i, i + 1) for i in range(count - 1)]
        backward = [(target, source) for source, target in forward]
        low = lax.ppermute(
            lax.slice_in_dim(block, block.shape[dim] - width, None, axis=dim), axis, forward
        )
        high = lax.ppermute(lax.slice_in_dim(block, 0, width, axis=dim), axis, backward)
        block = jnp.concatenate([low, block, high], axis=dim)
    return block


def apply_block(row_block, vectors, factor):
    inner_part = jnp.dot(
        vectors, row_block, precision=exact_mode, preferred_element_type=jnp.float32
    )
    inner_part = jnp.dot(
        factor, inner_part, precision=exact_mode, preferred_element_type=jnp.float32
    )
    return row_block - jnp.dot(
        vectors.T, inner_part, precision=exact_mode, preferred_element_type=jnp.float32
    )


def keep_same(operand):
    return operand


def per_device(singular_vectors, reflector_vectors, reflector_factors, sweep_bounds):
    row_count = lax.axis_size("row")
    owner_row = lax.axis_index("row")
    row_dev, col_count = singular_vectors.shape
    reflect = reflector_vectors.shape[3] // 2
    blocks_dev = row_dev // reflect
    sweep_count = reflector_vectors.shape[0]
    vectors_all, factors_all = (
        lax.all_gather(reflector_vectors, "col", axis=2, tiled=True),
        lax.all_gather(reflector_factors, "col", axis=2, tiled=True),
    )
    pieces = 4
    piece_cols = col_count // pieces
    unit_count = sweep_count * pieces
    steps_total = row_count - 1 + unit_count
    lag_steps = row_count - 1 - owner_row

    def one_step(step_id, state_pair):
        field_now, below_rows = state_pair
        unit_now = step_id - lag_steps
        active = (unit_now >= 0) & (unit_now < unit_count)
        unit_safe = jnp.clip(unit_now, 0, unit_count - 1)
        col_start = unit_safe % pieces * piece_cols
        sweep_id = unit_safe // pieces
        first_row = sweep_bounds[sweep_id, 0]
        last_row = sweep_bounds[sweep_id, 1]
        vec_sweep = lax.dynamic_index_in_dim(vectors_all, sweep_id, 0, keepdims=False)
        fac_sweep = lax.dynamic_index_in_dim(factors_all, sweep_id, 0, keepdims=False)

        def work(operand):
            field_in, below_in = operand
            own_part = lax.dynamic_slice_in_dim(field_in, col_start, piece_cols, 1)
            extended = jnp.concatenate([own_part, below_in], axis=0)

            def one_block(counter, current):
                local_id = blocks_dev - 1 - counter
                start_row = (owner_row * blocks_dev + local_id) * reflect
                is_live = (start_row >= first_row) & (start_row <= last_row)

                def update(matrix):
                    row_block = lax.dynamic_slice_in_dim(matrix, local_id * reflect, 2 * reflect, 0)
                    vectors = lax.dynamic_index_in_dim(vec_sweep, local_id, 0, keepdims=False)
                    factor = lax.dynamic_index_in_dim(fac_sweep, local_id, 0, keepdims=False)
                    row_block = apply_block(row_block, vectors, factor)
                    return lax.dynamic_update_slice_in_dim(matrix, row_block, local_id * reflect, 0)

                return lax.cond(is_live, update, keep_same, current)

            extended = lax.fori_loop(0, blocks_dev, one_block, extended)
            field_out = lax.dynamic_update_slice_in_dim(field_in, extended[:row_dev], col_start, 1)
            return (field_out, extended[row_dev:])

        field_now, returned = lax.cond(active, work, keep_same, (field_now, below_rows))
        top_rows = lax.dynamic_slice(field_now, (0, col_start), (reflect, piece_cols))
        message = jnp.concatenate([top_rows, returned], axis=0)
        padded = extended_2(message, (("row", 0),), reflect)
        from_left = padded[:reflect]
        below_next = padded[3 * reflect :]
        prior = unit_now - 1
        valid = (owner_row > 0) & (prior >= 0) & (prior < unit_count)
        prior_col = jnp.clip(prior, 0, unit_count - 1) % pieces * piece_cols
        current_top = lax.dynamic_slice(field_now, (0, prior_col), (reflect, piece_cols))
        field_now = lax.dynamic_update_slice(
            field_now, jnp.where(valid, from_left, current_top), (0, prior_col)
        )
        return (field_now, below_next)

    def two_steps(pair_id, state_pair):
        return one_step(2 * pair_id + 1, one_step(2 * pair_id, state_pair))

    below_start = jnp.zeros((reflect, piece_cols), jnp.float32)
    pair_count = (steps_total + 1) // 2
    result_field, below_last = lax.fori_loop(
        0, pair_count, two_steps, (singular_vectors, below_start)
    )
    return result_field


def solution(mesh):
    placed = (P("row", "col"), P(None, "row", "col", None), P(None, "row", "col", None), P())
    return jax.shard_map(
        per_device, mesh=mesh, in_specs=placed, out_specs=P("row", "col"), check_vma=False
    )
```

profile of v0, /device:TPU:1, one launch (start us, length us, event | category | flops | bytes accessed | tf_op | source)
XLA Modules:
  0.0 527.2 jit_solution(4495330475815302078)
XLA Ops:
  6.5 3.2 copy.45
  10.5 29.0 %all-gather.5.cloned.1.call-done = f32[2,2,256,256]{3,2,1,0:T(8,128)} async-done(((f32[2,2,64,256]{3,2,1,0:T(8,128)}), f32[2,2,256,256]{3,2,1,0:T(8,128)}) %all-gather.5.cloned.1.call-update) | async-done | bytes 1048592 | tf_op jit(solution)/shard_map/all_gather | solution.py:47
  39.5 46.9 %all-gather.3.cloned.1.call-done = f32[2,2,256,512]{3,2,1,0:T(8,128)} async-done(((f32[2,2,64,512]{3,2,1,0:T(8,128)}), f32[2,2,256,512]{3,2,1,0:T(8,128)}) %all-gather.3.cloned.1.call-update) | async-done | bytes 2097168 | tf_op jit(solution)/shard_map/all_gather | solution.py:46
  86.4 433.9 %while.66 = (s32[]{:T(128)}, f32[512,1024]{1,0:T(8,128)}, f32[256,256]{1,0:T(8,128)S(1)}, s32[]{:T(128)}, s32[2,2]{1,0:T(2,128)S(1)}, /*index=5*/f32[2,2,256,512...) while((s32[]{:T(128)}, f32[512,1024]{1,0:T(8,128)}, ...), condition=%wide.region_13.14_spmd, body=%wide.region_0.13_spmd.sunk | while | flops 2014052352 | bytes 39848304 | solution.py:110
  86.5 3.8 collective-permute-start
  90.3 3.3 collective-permute-done
  97.3 6.5 %collective-permute-done.1 = f32[256,256]{1,0:T(8,128)S(1)} collective-permute-done((f32[256,256]{1,0:T(8,128)S(1)}, f32[256,256]{1,0:T(8,128)S(1)}, u32[]{:S(2)}, u32[]{:S(2)}) %collective-permute-start.1) | collective-permute-done | bytes 262176 | tf_op jit(solution)/shard_map/while/body/eval_jaxpr/ppermute | solution.py:17
  105.8 3.3 collective-permute-done.2
  112.8 6.5 %collective-permute-done.3 = f32[256,256]{1,0:T(8,128)S(1)} collective-permute-done((f32[256,256]{1,0:T(8,128)S(1)}, f32[256,256]{1,0:T(8,128)S(1)}, u32[]{:S(2)}, u32[]{:S(2)}) %collective-permute-start.3) | collective-permute-done | bytes 262176 | tf_op jit(solution)/shard_map/while/body/eval_jaxpr/ppermute | solution.py:17
  121.2 3.3 collective-permute-done
  128.2 6.9 %collective-permute-done.1 = f32[256,256]{1,0:T(8,128)S(1)} collective-permute-done((f32[256,256]{1,0:T(8,128)S(1)}, f32[256,256]{1,0:T(8,128)S(1)}, u32[]{:S(2)}, u32[]{:S(2)}) %collective-permute-start.1) | collective-permute-done | bytes 262176 | tf_op jit(solution)/shard_map/while/body/eval_jaxpr/ppermute | solution.py:17
  135.1 13.0 %collective-permute-start.2 = (f32[256,256]{1,0:T(8,128)S(1)}, f32[256,256]{1,0:T(8,128)S(1)}, u32[]{:S(2)}, u32[]{:S(2)}) collective-permute-start(f32[256,256]{1,0:T(8,128)S(1)} %get-tuple-element.1135), channel_id=1, source_target_pairs={{0,4},{4,8},{8,12},{12,16},{16,20},{20,24},{24,28},{1,5},{5,9},{9,... | collective-permute-start | bytes 786440 | tf_op jit(solution)/shard_map/while/body/eval_jaxpr/ppermute | solution.py:14
  148.2 3.3 collective-permute-done.2
  155.2 21.6 %collective-permute-done.3 = f32[256,256]{1,0:T(8,128)S(1)} collective-permute-done((f32[256,256]{1,0:T(8,128)S(1)}, f32[256,256]{1,0:T(8,128)S(1)}, u32[]{:S(2)}, u32[]{:S(2)}) %collective-permute-start.3) | collective-permute-done | bytes 262176 | tf_op jit(solution)/shard_map/while/body/eval_jaxpr/ppermute | solution.py:17
  176.7 14.2 %collective-permute-start = (f32[256,256]{1,0:T(8,128)S(1)}, f32[256,256]{1,0:T(8,128)S(1)}, u32[]{:S(2)}, u32[]{:S(2)}) collective-permute-start(f32[256,256]{1,0:T(8,128)S(1)} %get-tuple-element.1131), channel_id=1, source_target_pairs={{0,4},{4,8},{8,12},{12,16},{16,20},{20,24},{24,28},{1,5},{5,9},{9,... | collective-permute-start | bytes 786440 | tf_op jit(solution)/shard_map/while/body/eval_jaxpr/ppermute | solution.py:14
  190.9 3.3 collective-permute-done
  197.9 21.6 %collective-permute-done.1 = f32[256,256]{1,0:T(8,128)S(1)} collective-permute-done((f32[256,256]{1,0:T(8,128)S(1)}, f32[256,256]{1,0:T(8,128)S(1)}, u32[]{:S(2)}, u32[]{:S(2)}) %collective-permute-start.1) | collective-permute-done | bytes 262176 | tf_op jit(solution)/shard_map/while/body/eval_jaxpr/ppermute | solution.py:17
  219.5 15.1 %collective-permute-start.2 = (f32[256,256]{1,0:T(8,128)S(1)}, f32[256,256]{1,0:T(8,128)S(1)}, u32[]{:S(2)}, u32[]{:S(2)}) collective-permute-start(f32[256,256]{1,0:T(8,128)S(1)} %get-tuple-element.1135), channel_id=1, source_target_pairs={{0,4},{4,8},{8,12},{12,16},{16,20},{20,24},{24,28},{1,5},{5,9},{9,... | collective-permute-start | bytes 786440 | tf_op jit(solution)/shard_map/while/body/eval_jaxpr/ppermute | solution.py:14
  234.6 3.3 collective-permute-done.2
  241.6 7.6 %collective-permute-done.3 = f32[256,256]{1,0:T(8,128)S(1)} collective-permute-done((f32[256,256]{1,0:T(8,128)S(1)}, f32[256,256]{1,0:T(8,128)S(1)}, u32[]{:S(2)}, u32[]{:S(2)}) %collective-permute-start.3) | collective-permute-done | bytes 262176 | tf_op jit(solution)/shard_map/while/body/eval_jaxpr/ppermute | solution.py:17
  249.2 13.3 %conditional.8 = ((f32[512,1024]{1,0:T(8,128)}, f32[256,256]{1,0:T(8,128)S(1)})) conditional(s32[]{:T(128)} %convert_element_type.45, (f32[512,1024]{1,0:T(8,128)}, f32[256,256]{1,0:T(8,128)S(1)}) %tuple.171, (s32[]{:T(128)}, f32[512,1024]{1,0:T(8,128)}, f32[256,256]{1,0:T(8,128)S(1)}, s32[]{:T(128)}, pred[]{:T(512)}, ...), branch_computations={%region_1.1_spmd, %region_2.6_spmd} | conditional | flops 1006960640 | bytes 16515680 | solution.py:90
  252.5 6.4 %while.64 = (s32[]{:T(128)}, f32[768,256]{1,0:T(8,128)S(1)}, s32[]{:T(128)}, s32[]{:T(128)}, s32[]{:T(128)}, /*index=5*/f32[2,256,512]{2,1,0:T(8,128)S(1)}, f32[2,256,256]{2,1,0:T(8,128)S(1)}, s32[]{:T(128)}, s32[]{:T(128)}) while((s32[]{:T(128)}, f32[768,256]{1,0:T(8,128)S(1)}, s32[]{:T(128)}, s32[]{:T(128)}, s32[]{:T(128)}, ...), condition=%wide.region_6.5_spmd, body=%wide.region_3.4_spmd.sunk | while | flops 1006764032 | bytes 3932463 | solution.py:86
  259.0 3.5 dynamic_update_slice.35
  264.4 3.3 collective-permute-done
  271.4 7.4 %collective-permute-done.1 = f32[256,256]{1,0:T(8,128)S(1)} collective-permute-done((f32[256,256]{1,0:T(8,128)S(1)}, f32[256,256]{1,0:T(8,128)S(1)}, u32[]{:S(2)}, u32[]{:S(2)}) %collective-permute-start.1) | collective-permute-done | bytes 262176 | tf_op jit(solution)/shard_map/while/body/eval_jaxpr/ppermute | solution.py:17
  278.8 13.3 %conditional.9 = ((f32[512,1024]{1,0:T(8,128)}, f32[256,256]{1,0:T(8,128)S(1)})) conditional(s32[]{:T(128)} %convert_element_type.44, (f32[512,1024]{1,0:T(8,128)}, f32[256,256]{1,0:T(8,128)S(1)}) %tuple.173, (s32[]{:T(128)}, f32[512,1024]{1,0:T(8,128)}, f32[256,256]{1,0:T(8,128)S(1)}, s32[]{:T(128)}, pred[]{:T(512)}, ...), branch_computations={%region_7.7_spmd, %region_8.12_spmd} | conditional | flops 1006960640 | bytes 16515680 | solution.py:90
  282.1 6.4 %while.65 = (s32[]{:T(128)}, f32[768,256]{1,0:T(8,128)S(1)}, s32[]{:T(128)}, s32[]{:T(128)}, s32[]{:T(128)}, /*index=5*/f32[2,256,512]{2,1,0:T(8,128)S(1)}, f32[2,256,256]{2,1,0:T(8,128)S(1)}, s32[]{:T(128)}, s32[]{:T(128)}) while((s32[]{:T(128)}, f32[768,256]{1,0:T(8,128)S(1)}, s32[]{:T(128)}, s32[]{:T(128)}, s32[]{:T(128)}, ...), condition=%wide.region_12.11_spmd, body=%wide.region_9.10_spmd.sunk | while | flops 1006764032 | bytes 3932463 | solution.py:86
  288.6 3.5 dynamic_update_slice.37
  294.1 3.3 collective-permute-done.2
  301.0 6.7 %collective-permute-done.3 = f32[256,256]{1,0:T(8,128)S(1)} collective-permute-done((f32[256,256]{1,0:T(8,128)S(1)}, f32[256,256]{1,0:T(8,128)S(1)}, u32[]{:S(2)}, u32[]{:S(2)}) %collective-permute-start.3) | collective-permute-done | bytes 262176 | tf_op jit(solution)/shard_map/while/body/eval_jaxpr/ppermute | solution.py:17
  307.7 13.3 %conditional.8 = ((f32[512,1024]{1,0:T(8,128)}, f32[256,256]{1,0:T(8,128)S(1)})) conditional(s32[]{:T(128)} %convert_element_type.45, (f32[512,1024]{1,0:T(8,128)}, f32[256,256]{1,0:T(8,128)S(1)}) %tuple.171, (s32[]{:T(128)}, f32[512,1024]{1,0:T(8,128)}, f32[256,256]{1,0:T(8,128)S(1)}, s32[]{:T(128)}, pred[]{:T(512)}, ...), branch_computations={%region_1.1_spmd, %region_2.6_spmd} | conditional | flops 1006960640 | bytes 16515680 | solution.py:90
  311.1 6.4 %while.64 = (s32[]{:T(128)}, f32[768,256]{1,0:T(8,128)S(1)}, s32[]{:T(128)}, s32[]{:T(128)}, s32[]{:T(128)}, /*index=5*/f32[2,256,512]{2,1,0:T(8,128)S(1)}, f32[2,256,256]{2,1,0:T(8,128)S(1)}, s32[]{:T(128)}, s32[]{:T(128)}) while((s32[]{:T(128)}, f32[768,256]{1,0:T(8,128)S(1)}, s32[]{:T(128)}, s32[]{:T(128)}, s32[]{:T(128)}, ...), condition=%wide.region_6.5_spmd, body=%wide.region_3.4_spmd.sunk | while | flops 1006764032 | bytes 3932463 | solution.py:86
  317.6 3.5 dynamic_update_slice.35
  323.0 3.3 collective-permute-done
  330.0 7.9 %collective-permute-done.1 = f32[256,256]{1,0:T(8,128)S(1)} collective-permute-done((f32[256,256]{1,0:T(8,128)S(1)}, f32[256,256]{1,0:T(8,128)S(1)}, u32[]{:S(2)}, u32[]{:S(2)}) %collective-permute-start.1) | collective-permute-done | bytes 262176 | tf_op jit(solution)/shard_map/while/body/eval_jaxpr/ppermute | solution.py:17
  337.9 12.6 %conditional.9 = ((f32[512,1024]{1,0:T(8,128)}, f32[256,256]{1,0:T(8,128)S(1)})) conditional(s32[]{:T(128)} %convert_element_type.44, (f32[512,1024]{1,0:T(8,128)}, f32[256,256]{1,0:T(8,128)S(1)}) %tuple.173, (s32[]{:T(128)}, f32[512,1024]{1,0:T(8,128)}, f32[256,256]{1,0:T(8,128)S(1)}, s32[]{:T(128)}, pred[]{:T(512)}, ...), branch_computations={%region_7.7_spmd, %region_8.12_spmd} | conditional | flops 1006960640 | bytes 16515680 | solution.py:90
  341.2 6.4 %while.65 = (s32[]{:T(128)}, f32[768,256]{1,0:T(8,128)S(1)}, s32[]{:T(128)}, s32[]{:T(128)}, s32[]{:T(128)}, /*index=5*/f32[2,256,512]{2,1,0:T(8,128)S(1)}, f32[2,256,256]{2,1,0:T(8,128)S(1)}, s32[]{:T(128)}, s32[]{:T(128)}) while((s32[]{:T(128)}, f32[768,256]{1,0:T(8,128)S(1)}, s32[]{:T(128)}, s32[]{:T(128)}, s32[]{:T(128)}, ...), condition=%wide.region_12.11_spmd, body=%wide.region_9.10_spmd.sunk | while | flops 1006764032 | bytes 3932463 | solution.py:86
  347.6 2.9 dynamic_update_slice.37
  353.0 3.3 collective-permute-done.2
  360.0 7.6 %collective-permute-done.3 = f32[256,256]{1,0:T(8,128)S(1)} collective-permute-done((f32[256,256]{1,0:T(8,128)S(1)}, f32[256,256]{1,0:T(8,128)S(1)}, u32[]{:S(2)}, u32[]{:S(2)}) %collective-permute-start.3) | collective-permute-done | bytes 262176 | tf_op jit(solution)/shard_map/while/body/eval_jaxpr/ppermute | solution.py:17
  367.5 13.3 %conditional.8 = ((f32[512,1024]{1,0:T(8,128)}, f32[256,256]{1,0:T(8,128)S(1)})) conditional(s32[]{:T(128)} %convert_element_type.45, (f32[512,1024]{1,0:T(8,128)}, f32[256,256]{1,0:T(8,128)S(1)}) %tuple.171, (s32[]{:T(128)}, f32[512,1024]{1,0:T(8,128)}, f32[256,256]{1,0:T(8,128)S(1)}, s32[]{:T(128)}, pred[]{:T(512)}, ...), branch_computations={%region_1.1_spmd, %region_2.6_spmd} | conditional | flops 1006960640 | bytes 16515680 | solution.py:90
  370.9 6.4 %while.64 = (s32[]{:T(128)}, f32[768,256]{1,0:T(8,128)S(1)}, s32[]{:T(128)}, s32[]{:T(128)}, s32[]{:T(128)}, /*index=5*/f32[2,256,512]{2,1,0:T(8,128)S(1)}, f32[2,256,256]{2,1,0:T(8,128)S(1)}, s32[]{:T(128)}, s32[]{:T(128)}) while((s32[]{:T(128)}, f32[768,256]{1,0:T(8,128)S(1)}, s32[]{:T(128)}, s32[]{:T(128)}, s32[]{:T(128)}, ...), condition=%wide.region_6.5_spmd, body=%wide.region_3.4_spmd.sunk | while | flops 1006764032 | bytes 3932463 | solution.py:86
  377.4 3.5 dynamic_update_slice.35
  382.8 3.3 collective-permute-done
  389.8 7.4 %collective-permute-done.1 = f32[256,256]{1,0:T(8,128)S(1)} collective-permute-done((f32[256,256]{1,0:T(8,128)S(1)}, f32[256,256]{1,0:T(8,128)S(1)}, u32[]{:S(2)}, u32[]{:S(2)}) %collective-permute-start.1) | collective-permute-done | bytes 262176 | tf_op jit(solution)/shard_map/while/body/eval_jaxpr/ppermute | solution.py:17
  397.2 13.3 %conditional.9 = ((f32[512,1024]{1,0:T(8,128)}, f32[256,256]{1,0:T(8,128)S(1)})) conditional(s32[]{:T(128)} %convert_element_type.44, (f32[512,1024]{1,0:T(8,128)}, f32[256,256]{1,0:T(8,128)S(1)}) %tuple.173, (s32[]{:T(128)}, f32[512,1024]{1,0:T(8,128)}, f32[256,256]{1,0:T(8,128)S(1)}, s32[]{:T(128)}, pred[]{:T(512)}, ...), branch_computations={%region_7.7_spmd, %region_8.12_spmd} | conditional | flops 1006960640 | bytes 16515680 | solution.py:90
  400.5 6.4 %while.65 = (s32[]{:T(128)}, f32[768,256]{1,0:T(8,128)S(1)}, s32[]{:T(128)}, s32[]{:T(128)}, s32[]{:T(128)}, /*index=5*/f32[2,256,512]{2,1,0:T(8,128)S(1)}, f32[2,256,256]{2,1,0:T(8,128)S(1)}, s32[]{:T(128)}, s32[]{:T(128)}) while((s32[]{:T(128)}, f32[768,256]{1,0:T(8,128)S(1)}, s32[]{:T(128)}, s32[]{:T(128)}, s32[]{:T(128)}, ...), condition=%wide.region_12.11_spmd, body=%wide.region_9.10_spmd.sunk | while | flops 1006764032 | bytes 3932463 | solution.py:86
  407.0 3.5 dynamic_update_slice.37
  412.4 3.3 collective-permute-done.2
  419.4 6.7 %collective-permute-done.3 = f32[256,256]{1,0:T(8,128)S(1)} collective-permute-done((f32[256,256]{1,0:T(8,128)S(1)}, f32[256,256]{1,0:T(8,128)S(1)}, u32[]{:S(2)}, u32[]{:S(2)}) %collective-permute-start.3) | collective-permute-done | bytes 262176 | tf_op jit(solution)/shard_map/while/body/eval_jaxpr/ppermute | solution.py:17
  426.1 13.3 %conditional.8 = ((f32[512,1024]{1,0:T(8,128)}, f32[256,256]{1,0:T(8,128)S(1)})) conditional(s32[]{:T(128)} %convert_element_type.45, (f32[512,1024]{1,0:T(8,128)}, f32[256,256]{1,0:T(8,128)S(1)}) %tuple.171, (s32[]{:T(128)}, f32[512,1024]{1,0:T(8,128)}, f32[256,256]{1,0:T(8,128)S(1)}, s32[]{:T(128)}, pred[]{:T(512)}, ...), branch_computations={%region_1.1_spmd, %region_2.6_spmd} | conditional | flops 1006960640 | bytes 16515680 | solution.py:90
  429.5 6.4 %while.64 = (s32[]{:T(128)}, f32[768,256]{1,0:T(8,128)S(1)}, s32[]{:T(128)}, s32[]{:T(128)}, s32[]{:T(128)}, /*index=5*/f32[2,256,512]{2,1,0:T(8,128)S(1)}, f32[2,256,256]{2,1,0:T(8,128)S(1)}, s32[]{:T(128)}, s32[]{:T(128)}) while((s32[]{:T(128)}, f32[768,256]{1,0:T(8,128)S(1)}, s32[]{:T(128)}, s32[]{:T(128)}, s32[]{:T(128)}, ...), condition=%wide.region_6.5_spmd, body=%wide.region_3.4_spmd.sunk | while | flops 1006764032 | bytes 3932463 | solution.py:86
  435.9 3.5 dynamic_update_slice.35
  441.4 3.3 collective-permute-done
  448.4 6.5 %collective-permute-done.1 = f32[256,256]{1,0:T(8,128)S(1)} collective-permute-done((f32[256,256]{1,0:T(8,128)S(1)}, f32[256,256]{1,0:T(8,128)S(1)}, u32[]{:S(2)}, u32[]{:S(2)}) %collective-permute-start.1) | collective-permute-done | bytes 262176 | tf_op jit(solution)/shard_map/while/body/eval_jaxpr/ppermute | solution.py:17
  454.9 12.6 %conditional.9 = ((f32[512,1024]{1,0:T(8,128)}, f32[256,256]{1,0:T(8,128)S(1)})) conditional(s32[]{:T(128)} %convert_element_type.44, (f32[512,1024]{1,0:T(8,128)}, f32[256,256]{1,0:T(8,128)S(1)}) %tuple.173, (s32[]{:T(128)}, f32[512,1024]{1,0:T(8,128)}, f32[256,256]{1,0:T(8,128)S(1)}, s32[]{:T(128)}, pred[]{:T(512)}, ...), branch_computations={%region_7.7_spmd, %region_8.12_spmd} | conditional | flops 1006960640 | bytes 16515680 | solution.py:90
  458.1 6.4 %while.65 = (s32[]{:T(128)}, f32[768,256]{1,0:T(8,128)S(1)}, s32[]{:T(128)}, s32[]{:T(128)}, s32[]{:T(128)}, /*index=5*/f32[2,256,512]{2,1,0:T(8,128)S(1)}, f32[2,256,256]{2,1,0:T(8,128)S(1)}, s32[]{:T(128)}, s32[]{:T(128)}) while((s32[]{:T(128)}, f32[768,256]{1,0:T(8,128)S(1)}, s32[]{:T(128)}, s32[]{:T(128)}, s32[]{:T(128)}, ...), condition=%wide.region_12.11_spmd, body=%wide.region_9.10_spmd.sunk | while | flops 1006764032 | bytes 3932463 | solution.py:86
  464.6 2.9 dynamic_update_slice.37
  469.4 3.3 collective-permute-done.2
  476.4 6.5 %collective-permute-done.3 = f32[256,256]{1,0:T(8,128)S(1)} collective-permute-done((f32[256,256]{1,0:T(8,128)S(1)}, f32[256,256]{1,0:T(8,128)S(1)}, u32[]{:S(2)}, u32[]{:S(2)}) %collective-permute-start.3) | collective-permute-done | bytes 262176 | tf_op jit(solution)/shard_map/while/body/eval_jaxpr/ppermute | solution.py:17
  484.9 8.0 %collective-permute-done = f32[256,256]{1,0:T(8,128)S(1)} collective-permute-done((f32[256,256]{1,0:T(8,128)S(1)}, f32[256,256]{1,0:T(8,128)S(1)}, u32[]{:S(2)}, u32[]{:S(2)}) %collective-permute-start) | collective-permute-done | bytes 262176 | tf_op jit(solution)/shard_map/while/body/eval_jaxpr/ppermute | solution.py:14
  496.7 8.2 %collective-permute-done.1 = f32[256,256]{1,0:T(8,128)S(1)} collective-permute-done((f32[256,256]{1,0:T(8,128)S(1)}, f32[256,256]{1,0:T(8,128)S(1)}, u32[]{:S(2)}, u32[]{:S(2)}) %collective-permute-start.1) | collective-permute-done | bytes 262176 | tf_op jit(solution)/shard_map/while/body/eval_jaxpr/ppermute | solution.py:17
  506.8 3.3 collective-permute-done.2
  513.8 6.5 %collective-permute-done.3 = f32[256,256]{1,0:T(8,128)S(1)} collective-permute-done((f32[256,256]{1,0:T(8,128)S(1)}, f32[256,256]{1,0:T(8,128)S(1)}, u32[]{:S(2)}, u32[]{:S(2)}) %collective-permute-start.3) | collective-permute-done | bytes 262176 | tf_op jit(solution)/shard_map/while/body/eval_jaxpr/ppermute | solution.py:17
  (195 shorter events, 175.3 us)
Async XLA Ops:
  6.5 79.9 %copy-start.2 = (s32[2,2]{1,0:T(2,128)S(1)}, s32[2,2]{1,0:T(2,128)}, u32[]{:S(2)}) copy-start(s32[2,2]{1,0:T(2,128)} %param.21) | copy-start | bytes 52
  6.5 32.9 %all-gather.5.cloned.1.call-start = ((), (), s32[]{:S(2)}) async-start(), calls=%async_computation.1 | async-start | bytes 1310720 | tf_op jit(solution)/shard_map/all_gather | solution.py:47
  9.7 76.7 %all-gather.3.cloned.1.call-start = ((), (), s32[]{:S(2)}) async-start(), calls=%async_computation | async-start | bytes 2621440 | tf_op jit(solution)/shard_map/all_gather | solution.py:46
  86.5 7.1 %collective-permute-start = (f32[256,256]{1,0:T(8,128)S(1)}, f32[256,256]{1,0:T(8,128)S(1)}, u32[]{:S(2)}, u32[]{:S(2)}) collective-permute-start(f32[256,256]{1,0:T(8,128)S(1)} %get-tuple-element.1131), channel_id=1, source_target_pairs={{0,4},{4,8},{8,12},{12,16},{16,20},{20,24},{24,28},{1,5},{5,9},{9,... | collective-permute-start | bytes 786440 | tf_op jit(solution)/shard_map/while/body/eval_jaxpr/ppermute | solution.py:14
  95.4 8.4 %collective-permute-start.1 = (f32[256,256]{1,0:T(8,128)S(1)}, f32[256,256]{1,0:T(8,128)S(1)}, u32[]{:S(2)}, u32[]{:S(2)}) collective-permute-start(f32[256,256]{1,0:T(8,128)S(1)} %get-tuple-element.1133), channel_id=1, source_target_pairs={{4,0},{8,4},{12,8},{16,12},{20,16},{24,20},{28,24},{5,1},{9,5},{13... | collective-permute-start | bytes 786440 | tf_op jit(solution)/shard_map/while/body/eval_jaxpr/ppermute | solution.py:17
  103.8 5.2 collective-permute-start.2
  110.8 8.4 %collective-permute-start.3 = (f32[256,256]{1,0:T(8,128)S(1)}, f32[256,256]{1,0:T(8,128)S(1)}, u32[]{:S(2)}, u32[]{:S(2)}) collective-permute-start(f32[256,256]{1,0:T(8,128)S(1)} %get-tuple-element.1137), channel_id=1, source_target_pairs={{4,0},{8,4},{12,8},{16,12},{20,16},{24,20},{28,24},{5,1},{9,5},{13... | collective-permute-start | bytes 786440 | tf_op jit(solution)/shard_map/while/body/eval_jaxpr/ppermute | solution.py:17
  119.3 5.2 collective-permute-start
  126.3 8.9 %collective-permute-start.1 = (f32[256,256]{1,0:T(8,128)S(1)}, f32[256,256]{1,0:T(8,128)S(1)}, u32[]{:S(2)}, u32[]{:S(2)}) collective-permute-start(f32[256,256]{1,0:T(8,128)S(1)} %get-tuple-element.1133), channel_id=1, source_target_pairs={{4,0},{8,4},{12,8},{16,12},{20,16},{24,20},{28,24},{5,1},{9,5},{13... | collective-permute-start | bytes 786440 | tf_op jit(solution)/shard_map/while/body/eval_jaxpr/ppermute | solution.py:17
  135.1 16.3 %collective-permute-start.2 = (f32[256,256]{1,0:T(8,128)S(1)}, f32[256,256]{1,0:T(8,128)S(1)}, u32[]{:S(2)}, u32[]{:S(2)}) collective-permute-start(f32[256,256]{1,0:T(8,128)S(1)} %get-tuple-element.1135), channel_id=1, source_target_pairs={{0,4},{4,8},{8,12},{12,16},{16,20},{20,24},{24,28},{1,5},{5,9},{9,... | collective-permute-start | bytes 786440 | tf_op jit(solution)/shard_map/while/body/eval_jaxpr/ppermute | solution.py:14
  153.2 23.5 %collective-permute-start.3 = (f32[256,256]{1,0:T(8,128)S(1)}, f32[256,256]{1,0:T(8,128)S(1)}, u32[]{:S(2)}, u32[]{:S(2)}) collective-permute-start(f32[256,256]{1,0:T(8,128)S(1)} %get-tuple-element.1137), channel_id=1, source_target_pairs={{4,0},{8,4},{12,8},{16,12},{20,16},{24,20},{28,24},{5,1},{9,5},{13... | collective-permute-start | bytes 786440 | tf_op jit(solution)/shard_map/while/body/eval_jaxpr/ppermute | solution.py:17
  176.7 17.5 %collective-permute-start = (f32[256,256]{1,0:T(8,128)S(1)}, f32[256,256]{1,0:T(8,128)S(1)}, u32[]{:S(2)}, u32[]{:S(2)}) collective-permute-start(f32[256,256]{1,0:T(8,128)S(1)} %get-tuple-element.1131), channel_id=1, source_target_pairs={{0,4},{4,8},{8,12},{12,16},{16,20},{20,24},{24,28},{1,5},{5,9},{9,... | collective-permute-start | bytes 786440 | tf_op jit(solution)/shard_map/while/body/eval_jaxpr/ppermute | solution.py:14
  196.0 23.5 %collective-permute-start.1 = (f32[256,256]{1,0:T(8,128)S(1)}, f32[256,256]{1,0:T(8,128)S(1)}, u32[]{:S(2)}, u32[]{:S(2)}) collective-permute-start(f32[256,256]{1,0:T(8,128)S(1)} %get-tuple-element.1133), channel_id=1, source_target_pairs={{4,0},{8,4},{12,8},{16,12},{20,16},{24,20},{28,24},{5,1},{9,5},{13... | collective-permute-start | bytes 786440 | tf_op jit(solution)/shard_map/while/body/eval_jaxpr/ppermute | solution.py:17
  219.5 18.4 %collective-permute-start.2 = (f32[256,256]{1,0:T(8,128)S(1)}, f32[256,256]{1,0:T(8,128)S(1)}, u32[]{:S(2)}, u32[]{:S(2)}) collective-permute-start(f32[256,256]{1,0:T(8,128)S(1)} %get-tuple-element.1135), channel_id=1, source_target_pairs={{0,4},{4,8},{8,12},{12,16},{16,20},{20,24},{24,28},{1,5},{5,9},{9,... | collective-permute-start | bytes 786440 | tf_op jit(solution)/shard_map/while/body/eval_jaxpr/ppermute | solution.py:14
  239.7 9.5 %collective-permute-start.3 = (f32[256,256]{1,0:T(8,128)S(1)}, f32[256,256]{1,0:T(8,128)S(1)}, u32[]{:S(2)}, u32[]{:S(2)}) collective-permute-start(f32[256,256]{1,0:T(8,128)S(1)} %get-tuple-element.1137), channel_id=1, source_target_pairs={{4,0},{8,4},{12,8},{16,12},{20,16},{24,20},{28,24},{5,1},{9,5},{13... | collective-permute-start | bytes 786440 | tf_op jit(solution)/shard_map/while/body/eval_jaxpr/ppermute | solution.py:17
  250.5 1.9 copy-start
  262.5 5.2 collective-permute-start
  269.5 9.3 %collective-permute-start.1 = (f32[256,256]{1,0:T(8,128)S(1)}, f32[256,256]{1,0:T(8,128)S(1)}, u32[]{:S(2)}, u32[]{:S(2)}) collective-permute-start(f32[256,256]{1,0:T(8,128)S(1)} %get-tuple-element.1133), channel_id=1, source_target_pairs={{4,0},{8,4},{12,8},{16,12},{20,16},{24,20},{28,24},{5,1},{9,5},{13... | collective-permute-start | bytes 786440 | tf_op jit(solution)/shard_map/while/body/eval_jaxpr/ppermute | solution.py:17
  280.1 1.9 copy-start.1
  292.1 5.2 collective-permute-start.2
  299.1 8.6 %collective-permute-start.3 = (f32[256,256]{1,0:T(8,128)S(1)}, f32[256,256]{1,0:T(8,128)S(1)}, u32[]{:S(2)}, u32[]{:S(2)}) collective-permute-start(f32[256,256]{1,0:T(8,128)S(1)} %get-tuple-element.1137), channel_id=1, source_target_pairs={{4,0},{8,4},{12,8},{16,12},{20,16},{24,20},{28,24},{5,1},{9,5},{13... | collective-permute-start | bytes 786440 | tf_op jit(solution)/shard_map/while/body/eval_jaxpr/ppermute | solution.py:17
  309.1 1.9 copy-start
  321.0 5.2 collective-permute-start
  328.1 9.8 %collective-permute-start.1 = (f32[256,256]{1,0:T(8,128)S(1)}, f32[256,256]{1,0:T(8,128)S(1)}, u32[]{:S(2)}, u32[]{:S(2)}) collective-permute-start(f32[256,256]{1,0:T(8,128)S(1)} %get-tuple-element.1133), channel_id=1, source_target_pairs={{4,0},{8,4},{12,8},{16,12},{20,16},{24,20},{28,24},{5,1},{9,5},{13... | collective-permute-start | bytes 786440 | tf_op jit(solution)/shard_map/while/body/eval_jaxpr/ppermute | solution.py:17
  339.1 1.9 copy-start.1
  350.5 5.7 %collective-permute-start.2 = (f32[256,256]{1,0:T(8,128)S(1)}, f32[256,256]{1,0:T(8,128)S(1)}, u32[]{:S(2)}, u32[]{:S(2)}) collective-permute-start(f32[256,256]{1,0:T(8,128)S(1)} %get-tuple-element.1135), channel_id=1, source_target_pairs={{0,4},{4,8},{8,12},{12,16},{16,20},{20,24},{24,28},{1,5},{5,9},{9,... | collective-permute-start | bytes 786440 | tf_op jit(solution)/shard_map/while/body/eval_jaxpr/ppermute | solution.py:14
  358.0 9.5 %collective-permute-start.3 = (f32[256,256]{1,0:T(8,128)S(1)}, f32[256,256]{1,0:T(8,128)S(1)}, u32[]{:S(2)}, u32[]{:S(2)}) collective-permute-start(f32[256,256]{1,0:T(8,128)S(1)} %get-tuple-element.1137), channel_id=1, source_target_pairs={{4,0},{8,4},{12,8},{16,12},{20,16},{24,20},{28,24},{5,1},{9,5},{13... | collective-permute-start | bytes 786440 | tf_op jit(solution)/shard_map/while/body/eval_jaxpr/ppermute | solution.py:17
  368.9 1.9 copy-start
  380.9 5.2 collective-permute-start
  387.9 9.3 %collective-permute-start.1 = (f32[256,256]{1,0:T(8,128)S(1)}, f32[256,256]{1,0:T(8,128)S(1)}, u32[]{:S(2)}, u32[]{:S(2)}) collective-permute-start(f32[256,256]{1,0:T(8,128)S(1)} %get-tuple-element.1133), channel_id=1, source_target_pairs={{4,0},{8,4},{12,8},{16,12},{20,16},{24,20},{28,24},{5,1},{9,5},{13... | collective-permute-start | bytes 786440 | tf_op jit(solution)/shard_map/while/body/eval_jaxpr/ppermute | solution.py:17
  398.5 1.9 copy-start.1
  410.5 5.2 collective-permute-start.2
  417.5 8.6 %collective-permute-start.3 = (f32[256,256]{1,0:T(8,128)S(1)}, f32[256,256]{1,0:T(8,128)S(1)}, u32[]{:S(2)}, u32[]{:S(2)}) collective-permute-start(f32[256,256]{1,0:T(8,128)S(1)} %get-tuple-element.1137), channel_id=1, source_target_pairs={{4,0},{8,4},{12,8},{16,12},{20,16},{24,20},{28,24},{5,1},{9,5},{13... | collective-permute-start | bytes 786440 | tf_op jit(solution)/shard_map/while/body/eval_jaxpr/ppermute | solution.py:17
  427.5 1.9 copy-start
  439.4 5.2 collective-permute-start
  446.4 8.4 %collective-permute-start.1 = (f32[256,256]{1,0:T(8,128)S(1)}, f32[256,256]{1,0:T(8,128)S(1)}, u32[]{:S(2)}, u32[]{:S(2)}) collective-permute-start(f32[256,256]{1,0:T(8,128)S(1)} %get-tuple-element.1133), channel_id=1, source_target_pairs={{4,0},{8,4},{12,8},{16,12},{20,16},{24,20},{28,24},{5,1},{9,5},{13... | collective-permute-start | bytes 786440 | tf_op jit(solution)/shard_map/while/body/eval_jaxpr/ppermute | solution.py:17
  456.1 1.9 copy-start.1
  467.5 5.2 collective-permute-start.2
  474.5 8.4 %collective-permute-start.3 = (f32[256,256]{1,0:T(8,128)S(1)}, f32[256,256]{1,0:T(8,128)S(1)}, u32[]{:S(2)}, u32[]{:S(2)}) collective-permute-start(f32[256,256]{1,0:T(8,128)S(1)} %get-tuple-element.1137), channel_id=1, source_target_pairs={{4,0},{8,4},{12,8},{16,12},{20,16},{24,20},{28,24},{5,1},{9,5},{13... | collective-permute-start | bytes 786440 | tf_op jit(solution)/shard_map/while/body/eval_jaxpr/ppermute | solution.py:17
  482.9 9.9 %collective-permute-start = (f32[256,256]{1,0:T(8,128)S(1)}, f32[256,256]{1,0:T(8,128)S(1)}, u32[]{:S(2)}, u32[]{:S(2)}) collective-permute-start(f32[256,256]{1,0:T(8,128)S(1)} %get-tuple-element.1131), channel_id=1, source_target_pairs={{0,4},{4,8},{8,12},{12,16},{16,20},{20,24},{24,28},{1,5},{5,9},{9,... | collective-permute-start | bytes 786440 | tf_op jit(solution)/shard_map/while/body/eval_jaxpr/ppermute | solution.py:14
  494.6 10.3 %collective-permute-start.1 = (f32[256,256]{1,0:T(8,128)S(1)}, f32[256,256]{1,0:T(8,128)S(1)}, u32[]{:S(2)}, u32[]{:S(2)}) collective-permute-start(f32[256,256]{1,0:T(8,128)S(1)} %get-tuple-element.1133), channel_id=1, source_target_pairs={{4,0},{8,4},{12,8},{16,12},{20,16},{24,20},{28,24},{5,1},{9,5},{13... | collective-permute-start | bytes 786440 | tf_op jit(solution)/shard_map/while/body/eval_jaxpr/ppermute | solution.py:17
  504.9 5.2 collective-permute-start.2
  511.9 8.4 %collective-permute-start.3 = (f32[256,256]{1,0:T(8,128)S(1)}, f32[256,256]{1,0:T(8,128)S(1)}, u32[]{:S(2)}, u32[]{:S(2)}) collective-permute-start(f32[256,256]{1,0:T(8,128)S(1)} %get-tuple-element.1137), channel_id=1, source_target_pairs={{4,0},{8,4},{12,8},{16,12},{20,16},{24,20},{28,24},{5,1},{9,5},{13... | collective-permute-start | bytes 786440 | tf_op jit(solution)/shard_map/while/body/eval_jaxpr/ppermute | solution.py:17
Sparse Core Ops, SparseCore 0:
  9.9 29.5 all-gather.4
  41.0 45.3 all-gather.2
where the time goes:
time: 530 us; the launch traced here: 527 us
  waiting for transfers between devices  276 us (52%)
  starting transfers between devices  100 us (19%)
  local copies, waits for them, and re-layouts  55.8 us (11%)
  matrix products  32.2 us (6%)
  other arithmetic  29 us (5%)
  loops' own time  20.7 us (4%)
  between operations  13.4 us (3%)
    ppermute x16, waiting for transfers between devices, extended_2(): lax.ppermute(lax.slice_in_dim(block, 0, width, axis=dim), axis, backward)  142 us
    ppermute x16, starting transfers between devices, extended_2(): lax.ppermute(lax.slice_in_dim(block, block.shape[dim] - width, None, axis...  69.6 us
    ppermute x16, waiting for transfers between devices, extended_2(): lax.ppermute(lax.slice_in_dim(block, block.shape[dim] - width, None, axis...  57.1 us
    all_gather x1, waiting for transfers between devices, per_device(): lax.all_gather(reflector_vectors, 'col', axis=2, tiled=True)  46.9 us
    ppermute x16, starting transfers between devices, extended_2(): lax.ppermute(lax.slice_in_dim(block, 0, width, axis=dim), axis, backward)  30.7 us
    all_gather x1, waiting for transfers between devices, per_device(): lax.all_gather(reflector_factors, 'col', axis=2, tiled=True)  29 us
    dynamic_slice x16, other arithmetic, one_step(): lax.dynamic_slice(field_now, (0, col_start), (reflect, piece_cols))  28.5 us
    dynamic_update_slice x8, local copies, waits for them, and re-layouts, work(): lax.dynamic_update_slice_in_dim(field_in, extended[:row_dev], col_start, 1)  26.5 us
  transfers between devices with their start and end apart: 34, of which 34 were waited for; matrix products, arithmetic and copies ran while one was open for 0% of the time, Pallas kernels for 0%

commit v1 on v0

--- a/solution.py
+++ b/solution.py
@@ -4,6 +4,14 @@
 from jax.sharding import PartitionSpec as P
 
 exact_mode = lax.Precision.HIGHEST
+
+
+def gather_from_all(shard, axis, dim):
+    size = lax.axis_size(axis)
+    repeats = [size if d == dim else 1 for d in range(shard.ndim)]
+    return lax.all_to_all(
+        jnp.tile(shard, repeats), axis, split_axis=dim, concat_axis=dim, tiled=True
+    )
 
 
 def extended_2(block, sides, width):
@@ -44,7 +52,7 @@
     sweep_count = reflector_vectors.shape[0]
     vectors_all, factors_all = (
         lax.all_gather(reflector_vectors, "col", axis=2, tiled=True),
-        lax.all_gather(reflector_factors, "col", axis=2, tiled=True),
+        gather_from_all(reflector_factors, "col", 2),
     )
     pieces = 4
     piece_cols = col_count // pieces

time: 530 us -> 524 us (0.989)
  waiting for transfers between devices: 276 us -> 260 us
  starting transfers between devices: 100 us -> 106 us
    all_to_all x0 -> x1, waiting for transfers between devices: none -> 47.4 us  [gather_from_all(): lax.all_to_all(jnp.tile(shard, repeats), axis, split_axis=dim, concat_axi...]
    all_gather x1, waiting for transfers between devices: 46.9 us -> 12.8 us  [per_device(): lax.all_gather(reflector_vectors, 'col', axis=2, tiled=True)]
    all_gather x1 -> x0, waiting for transfers between devices: 29 us -> none  [per_device(): lax.all_gather(reflector_factors, 'col', axis=2, tiled=True)]
    all_to_all x0 -> x1, starting transfers between devices: none -> 5.54 us  [gather_from_all(): lax.all_to_all(jnp.tile(shard, repeats), axis, split_axis=dim, concat_axi...]
where the time goes in v1:
time: 524 us; the launch traced here: 521 us
  waiting for transfers between devices  260 us (50%)
  starting transfers between devices  106 us (20%)
  local copies, waits for them, and re-layouts  58.2 us (11%)
  matrix products  32.2 us (6%)
  other arithmetic  29 us (6%)
  loops' own time  21.8 us (4%)
  between operations  13.4 us (3%)
    ppermute x16, waiting for transfers between devices, extended_2(): lax.ppermute(lax.slice_in_dim(block, 0, width, axis=dim), axis, backward)  143 us
    ppermute x16, starting transfers between devices, extended_2(): lax.ppermute(lax.slice_in_dim(block, block.shape[dim] - width, None, axis...  70 us
    ppermute x16, waiting for transfers between devices, extended_2(): lax.ppermute(lax.slice_in_dim(block, block.shape[dim] - width, None, axis...  57.4 us
    all_to_all x1, waiting for transfers between devices, gather_from_all(): lax.all_to_all(jnp.tile(shard, repeats), axis, split_axis=dim, concat_axi...  47.4 us
    ppermute x16, starting transfers between devices, extended_2(): lax.ppermute(lax.slice_in_dim(block, 0, width, axis=dim), axis, backward)  30.7 us
    dynamic_slice x16, other arithmetic, one_step(): lax.dynamic_slice(field_now, (0, col_start), (reflect, piece_cols))  28.5 us
    dynamic_update_slice x8, local copies, waits for them, and re-layouts, work(): lax.dynamic_update_slice_in_dim(field_in, extended[:row_dev], col_start, 1)  26.5 us
    another operation x8, loops' own time, work(): extended = lax.fori_loop(0, blocks_dev, one_block, extended)  19.6 us
  transfers between devices with their start and end apart: 34, of which 34 were waited for; matrix products, arithmetic and copies ran while one was open for 0% of the time, Pallas kernels for 0%

profile of v1, /device:TPU:1, one launch (start us, length us, event | category | flops | bytes accessed | tf_op | source)
XLA Modules:
  0.0 521.3 jit_solution(10274150501410048753)
XLA Ops:
  6.5 3.2 copy.47
  11.3 5.5 %all-to-all-start = ((f32[2,2,256,256]{3,1,0,2:T(2,128)}), f32[2,2,256,256]{3,1,0,2:T(2,128)S(1)}, u32[]{:S(2)}, u32[]{:S(2)}) async-start(f32[2,2,256,256]{3,1,0,2:T(2,128)} %bitcast.12), calls=%async_computation | async-start | bytes 2097152 | tf_op jit(solution)/shard_map/all_to_all | solution.py:12
  16.8 47.4 %all-to-all-done = f32[2,2,256,256]{3,1,0,2:T(2,128)S(1)} async-done(((f32[2,2,256,256]{3,1,0,2:T(2,128)}), f32[2,2,256,256]{3,1,0,2:T(2,128)S(1)}, u32[]{:S(2)}, u32[]{:S(2)}) %all-to-all-start) | async-done | bytes 1048608 | tf_op jit(solution)/shard_map/all_to_all | solution.py:12
  64.4 12.8 %all-gather.2.cloned.1.call-done = f32[2,2,256,512]{3,2,1,0:T(8,128)} async-done(((f32[2,2,64,512]{3,2,1,0:T(8,128)}), f32[2,2,256,512]{3,2,1,0:T(8,128)}) %all-gather.2.cloned.1.call-update) | async-done | bytes 2097168 | tf_op jit(solution)/shard_map/all_gather | solution.py:54
  77.2 437.3 %while.66 = (s32[]{:T(128)}, f32[512,1024]{1,0:T(8,128)}, f32[256,256]{1,0:T(8,128)S(1)}, s32[]{:T(128)}, s32[2,2]{1,0:T(2,128)S(1)}, /*index=5*/f32[2,2,256,512...) while((s32[]{:T(128)}, f32[512,1024]{1,0:T(8,128)}, ...), condition=%wide.region_13.14_spmd, body=%wide.region_0.13_spmd.sunk | while | flops 2014052352 | bytes 31459644 | solution.py:118
  77.3 3.5 collective-permute-start
  80.8 3.3 collective-permute-done
  87.8 6.5 %collective-permute-done.1 = f32[256,256]{1,0:T(8,128)S(1)} collective-permute-done((f32[256,256]{1,0:T(8,128)S(1)}, f32[256,256]{1,0:T(8,128)S(1)}, u32[]{:S(2)}, u32[]{:S(2)}) %collective-permute-start.1) | collective-permute-done | bytes 262176 | tf_op jit(solution)/shard_map/while/body/eval_jaxpr/ppermute | solution.py:25
  96.2 3.3 collective-permute-done.2
  103.2 6.5 %collective-permute-done.3 = f32[256,256]{1,0:T(8,128)S(1)} collective-permute-done((f32[256,256]{1,0:T(8,128)S(1)}, f32[256,256]{1,0:T(8,128)S(1)}, u32[]{:S(2)}, u32[]{:S(2)}) %collective-permute-start.3) | collective-permute-done | bytes 262176 | tf_op jit(solution)/shard_map/while/body/eval_jaxpr/ppermute | solution.py:25
  111.6 3.3 collective-permute-done
  118.6 7.6 %collective-permute-done.1 = f32[256,256]{1,0:T(8,128)S(1)} collective-permute-done((f32[256,256]{1,0:T(8,128)S(1)}, f32[256,256]{1,0:T(8,128)S(1)}, u32[]{:S(2)}, u32[]{:S(2)}) %collective-permute-start.1) | collective-permute-done | bytes 262176 | tf_op jit(solution)/shard_map/while/body/eval_jaxpr/ppermute | solution.py:25
  126.2 13.3 %collective-permute-start.2 = (f32[256,256]{1,0:T(8,128)S(1)}, f32[256,256]{1,0:T(8,128)S(1)}, u32[]{:S(2)}, u32[]{:S(2)}) collective-permute-start(f32[256,256]{1,0:T(8,128)S(1)} %get-tuple-element.1144), channel_id=1, source_target_pairs={{0,4},{4,8},{8,12},{12,16},{16,20},{20,24},{24,28},{1,5},{5,9},{9,... | collective-permute-start | bytes 786440 | tf_op jit(solution)/shard_map/while/body/eval_jaxpr/ppermute | solution.py:22
  139.5 3.3 collective-permute-done.2
  146.5 21.8 %collective-permute-done.3 = f32[256,256]{1,0:T(8,128)S(1)} collective-permute-done((f32[256,256]{1,0:T(8,128)S(1)}, f32[256,256]{1,0:T(8,128)S(1)}, u32[]{:S(2)}, u32[]{:S(2)}) %collective-permute-start.3) | collective-permute-done | bytes 262176 | tf_op jit(solution)/shard_map/while/body/eval_jaxpr/ppermute | solution.py:25
  168.3 14.4 %collective-permute-start = (f32[256,256]{1,0:T(8,128)S(1)}, f32[256,256]{1,0:T(8,128)S(1)}, u32[]{:S(2)}, u32[]{:S(2)}) collective-permute-start(f32[256,256]{1,0:T(8,128)S(1)} %get-tuple-element.1140), channel_id=1, source_target_pairs={{0,4},{4,8},{8,12},{12,16},{16,20},{20,24},{24,28},{1,5},{5,9},{9,... | collective-permute-start | bytes 786440 | tf_op jit(solution)/shard_map/while/body/eval_jaxpr/ppermute | solution.py:22
  182.7 3.3 collective-permute-done
  189.7 21.8 %collective-permute-done.1 = f32[256,256]{1,0:T(8,128)S(1)} collective-permute-done((f32[256,256]{1,0:T(8,128)S(1)}, f32[256,256]{1,0:T(8,128)S(1)}, u32[]{:S(2)}, u32[]{:S(2)}) %collective-permute-start.1) | collective-permute-done | bytes 262176 | tf_op jit(solution)/shard_map/while/body/eval_jaxpr/ppermute | solution.py:25
  211.5 15.3 %collective-permute-start.2 = (f32[256,256]{1,0:T(8,128)S(1)}, f32[256,256]{1,0:T(8,128)S(1)}, u32[]{:S(2)}, u32[]{:S(2)}) collective-permute-start(f32[256,256]{1,0:T(8,128)S(1)} %get-tuple-element.1144), channel_id=1, source_target_pairs={{0,4},{4,8},{8,12},{12,16},{16,20},{20,24},{24,28},{1,5},{5,9},{9,... | collective-permute-start | bytes 786440 | tf_op jit(solution)/shard_map/while/body/eval_jaxpr/ppermute | solution.py:22
  226.8 3.3 collective-permute-done.2
  233.8 7.6 %collective-permute-done.3 = f32[256,256]{1,0:T(8,128)S(1)} collective-permute-done((f32[256,256]{1,0:T(8,128)S(1)}, f32[256,256]{1,0:T(8,128)S(1)}, u32[]{:S(2)}, u32[]{:S(2)}) %collective-permute-start.3) | collective-permute-done | bytes 262176 | tf_op jit(solution)/shard_map/while/body/eval_jaxpr/ppermute | solution.py:25
  241.4 13.5 %conditional.8 = ((f32[512,1024]{1,0:T(8,128)}, f32[256,256]{1,0:T(8,128)S(1)})) conditional(s32[]{:T(128)} %convert_element_type.45, (f32[512,1024]{1,0:T(8,128)}, f32[256,256]{1,0:T(8,128)S(1)}) %tuple.172, (s32[]{:T(128)}, f32[512,1024]{1,0:T(8,128)}, f32[256,256]{1,0:T(8,128)S(1)}, s32[]{:T(128)}, pred[]{:T(512)}, ...), branch_computations={%region_1.1_spmd, %region_2.6_spmd} | conditional | flops 1006960640 | bytes 12321348 | solution.py:98
  244.8 6.6 %while.64 = (s32[]{:T(128)}, f32[768,256]{1,0:T(8,128)S(1)}, s32[]{:T(128)}, s32[]{:T(128)}, s32[]{:T(128)}, /*index=5*/f32[2,256,512]{2,1,0:T(8,128)S(1)}, f32[2,256,256]{2,1,0:T(8,128)S(1)}, s32[]{:T(128)}, s32[]{:T(128)}) while((s32[]{:T(128)}, f32[768,256]{1,0:T(8,128)S(1)}, s32[]{:T(128)}, s32[]{:T(128)}, s32[]{:T(128)}, ...), condition=%wide.region_6.5_spmd, body=%wide.region_3.4_spmd.sunk | while | flops 1006764032 | bytes 3932463 | solution.py:94
  251.5 3.5 dynamic_update_slice.35
  256.9 3.3 collective-permute-done
  263.9 7.4 %collective-permute-done.1 = f32[256,256]{1,0:T(8,128)S(1)} collective-permute-done((f32[256,256]{1,0:T(8,128)S(1)}, f32[256,256]{1,0:T(8,128)S(1)}, u32[]{:S(2)}, u32[]{:S(2)}) %collective-permute-start.1) | collective-permute-done | bytes 262176 | tf_op jit(solution)/shard_map/while/body/eval_jaxpr/ppermute | solution.py:25
  271.3 13.5 %conditional.9 = ((f32[512,1024]{1,0:T(8,128)}, f32[256,256]{1,0:T(8,128)S(1)})) conditional(s32[]{:T(128)} %convert_element_type.44, (f32[512,1024]{1,0:T(8,128)}, f32[256,256]{1,0:T(8,128)S(1)}) %tuple.174, (s32[]{:T(128)}, f32[512,1024]{1,0:T(8,128)}, f32[256,256]{1,0:T(8,128)S(1)}, s32[]{:T(128)}, pred[]{:T(512)}, ...), branch_computations={%region_7.7_spmd, %region_8.12_spmd} | conditional | flops 1006960640 | bytes 12321348 | solution.py:98
  274.7 6.6 %while.65 = (s32[]{:T(128)}, f32[768,256]{1,0:T(8,128)S(1)}, s32[]{:T(128)}, s32[]{:T(128)}, s32[]{:T(128)}, /*index=5*/f32[2,256,512]{2,1,0:T(8,128)S(1)}, f32[2,256,256]{2,1,0:T(8,128)S(1)}, s32[]{:T(128)}, s32[]{:T(128)}) while((s32[]{:T(128)}, f32[768,256]{1,0:T(8,128)S(1)}, s32[]{:T(128)}, s32[]{:T(128)}, s32[]{:T(128)}, ...), condition=%wide.region_12.11_spmd, body=%wide.region_9.10_spmd.sunk | while | flops 1006764032 | bytes 3932463 | solution.py:94
  281.3 3.5 dynamic_update_slice.37
  286.8 3.3 collective-permute-done.2
  293.7 6.7 %collective-permute-done.3 = f32[256,256]{1,0:T(8,128)S(1)} collective-permute-done((f32[256,256]{1,0:T(8,128)S(1)}, f32[256,256]{1,0:T(8,128)S(1)}, u32[]{:S(2)}, u32[]{:S(2)}) %collective-permute-start.3) | collective-permute-done | bytes 262176 | tf_op jit(solution)/shard_map/while/body/eval_jaxpr/ppermute | solution.py:25
  300.5 13.5 %conditional.8 = ((f32[512,1024]{1,0:T(8,128)}, f32[256,256]{1,0:T(8,128)S(1)})) conditional(s32[]{:T(128)} %convert_element_type.45, (f32[512,1024]{1,0:T(8,128)}, f32[256,256]{1,0:T(8,128)S(1)}) %tuple.172, (s32[]{:T(128)}, f32[512,1024]{1,0:T(8,128)}, f32[256,256]{1,0:T(8,128)S(1)}, s32[]{:T(128)}, pred[]{:T(512)}, ...), branch_computations={%region_1.1_spmd, %region_2.6_spmd} | conditional | flops 1006960640 | bytes 12321348 | solution.py:98
  303.9 6.6 %while.64 = (s32[]{:T(128)}, f32[768,256]{1,0:T(8,128)S(1)}, s32[]{:T(128)}, s32[]{:T(128)}, s32[]{:T(128)}, /*index=5*/f32[2,256,512]{2,1,0:T(8,128)S(1)}, f32[2,256,256]{2,1,0:T(8,128)S(1)}, s32[]{:T(128)}, s32[]{:T(128)}) while((s32[]{:T(128)}, f32[768,256]{1,0:T(8,128)S(1)}, s32[]{:T(128)}, s32[]{:T(128)}, s32[]{:T(128)}, ...), condition=%wide.region_6.5_spmd, body=%wide.region_3.4_spmd.sunk | while | flops 1006764032 | bytes 3932463 | solution.py:94
  310.5 3.5 dynamic_update_slice.35
  316.0 3.3 collective-permute-done
  323.0 7.9 %collective-permute-done.1 = f32[256,256]{1,0:T(8,128)S(1)} collective-permute-done((f32[256,256]{1,0:T(8,128)S(1)}, f32[256,256]{1,0:T(8,128)S(1)}, u32[]{:S(2)}, u32[]{:S(2)}) %collective-permute-start.1) | collective-permute-done | bytes 262176 | tf_op jit(solution)/shard_map/while/body/eval_jaxpr/ppermute | solution.py:25
  330.9 12.8 %conditional.9 = ((f32[512,1024]{1,0:T(8,128)}, f32[256,256]{1,0:T(8,128)S(1)})) conditional(s32[]{:T(128)} %convert_element_type.44, (f32[512,1024]{1,0:T(8,128)}, f32[256,256]{1,0:T(8,128)S(1)}) %tuple.174, (s32[]{:T(128)}, f32[512,1024]{1,0:T(8,128)}, f32[256,256]{1,0:T(8,128)S(1)}, s32[]{:T(128)}, pred[]{:T(512)}, ...), branch_computations={%region_7.7_spmd, %region_8.12_spmd} | conditional | flops 1006960640 | bytes 12321348 | solution.py:98
  334.2 6.6 %while.65 = (s32[]{:T(128)}, f32[768,256]{1,0:T(8,128)S(1)}, s32[]{:T(128)}, s32[]{:T(128)}, s32[]{:T(128)}, /*index=5*/f32[2,256,512]{2,1,0:T(8,128)S(1)}, f32[2,256,256]{2,1,0:T(8,128)S(1)}, s32[]{:T(128)}, s32[]{:T(128)}) while((s32[]{:T(128)}, f32[768,256]{1,0:T(8,128)S(1)}, s32[]{:T(128)}, s32[]{:T(128)}, s32[]{:T(128)}, ...), condition=%wide.region_12.11_spmd, body=%wide.region_9.10_spmd.sunk | while | flops 1006764032 | bytes 3932463 | solution.py:94
  340.8 2.9 dynamic_update_slice.37
  346.2 3.3 collective-permute-done.2
  353.2 7.6 %collective-permute-done.3 = f32[256,256]{1,0:T(8,128)S(1)} collective-permute-done((f32[256,256]{1,0:T(8,128)S(1)}, f32[256,256]{1,0:T(8,128)S(1)}, u32[]{:S(2)}, u32[]{:S(2)}) %collective-permute-start.3) | collective-permute-done | bytes 262176 | tf_op jit(solution)/shard_map/while/body/eval_jaxpr/ppermute | solution.py:25
  360.7 13.5 %conditional.8 = ((f32[512,1024]{1,0:T(8,128)}, f32[256,256]{1,0:T(8,128)S(1)})) conditional(s32[]{:T(128)} %convert_element_type.45, (f32[512,1024]{1,0:T(8,128)}, f32[256,256]{1,0:T(8,128)S(1)}) %tuple.172, (s32[]{:T(128)}, f32[512,1024]{1,0:T(8,128)}, f32[256,256]{1,0:T(8,128)S(1)}, s32[]{:T(128)}, pred[]{:T(512)}, ...), branch_computations={%region_1.1_spmd, %region_2.6_spmd} | conditional | flops 1006960640 | bytes 12321348 | solution.py:98
  364.2 6.6 %while.64 = (s32[]{:T(128)}, f32[768,256]{1,0:T(8,128)S(1)}, s32[]{:T(128)}, s32[]{:T(128)}, s32[]{:T(128)}, /*index=5*/f32[2,256,512]{2,1,0:T(8,128)S(1)}, f32[2,256,256]{2,1,0:T(8,128)S(1)}, s32[]{:T(128)}, s32[]{:T(128)}) while((s32[]{:T(128)}, f32[768,256]{1,0:T(8,128)S(1)}, s32[]{:T(128)}, s32[]{:T(128)}, s32[]{:T(128)}, ...), condition=%wide.region_6.5_spmd, body=%wide.region_3.4_spmd.sunk | while | flops 1006764032 | bytes 3932463 | solution.py:94
  370.8 3.5 dynamic_update_slice.35
  376.2 3.3 collective-permute-done
  383.2 7.4 %collective-permute-done.1 = f32[256,256]{1,0:T(8,128)S(1)} collective-permute-done((f32[256,256]{1,0:T(8,128)S(1)}, f32[256,256]{1,0:T(8,128)S(1)}, u32[]{:S(2)}, u32[]{:S(2)}) %collective-permute-start.1) | collective-permute-done | bytes 262176 | tf_op jit(solution)/shard_map/while/body/eval_jaxpr/ppermute | solution.py:25
  390.6 13.5 %conditional.9 = ((f32[512,1024]{1,0:T(8,128)}, f32[256,256]{1,0:T(8,128)S(1)})) conditional(s32[]{:T(128)} %convert_element_type.44, (f32[512,1024]{1,0:T(8,128)}, f32[256,256]{1,0:T(8,128)S(1)}) %tuple.174, (s32[]{:T(128)}, f32[512,1024]{1,0:T(8,128)}, f32[256,256]{1,0:T(8,128)S(1)}, s32[]{:T(128)}, pred[]{:T(512)}, ...), branch_computations={%region_7.7_spmd, %region_8.12_spmd} | conditional | flops 1006960640 | bytes 12321348 | solution.py:98
  394.0 6.6 %while.65 = (s32[]{:T(128)}, f32[768,256]{1,0:T(8,128)S(1)}, s32[]{:T(128)}, s32[]{:T(128)}, s32[]{:T(128)}, /*index=5*/f32[2,256,512]{2,1,0:T(8,128)S(1)}, f32[2,256,256]{2,1,0:T(8,128)S(1)}, s32[]{:T(128)}, s32[]{:T(128)}) while((s32[]{:T(128)}, f32[768,256]{1,0:T(8,128)S(1)}, s32[]{:T(128)}, s32[]{:T(128)}, s32[]{:T(128)}, ...), condition=%wide.region_12.11_spmd, body=%wide.region_9.10_spmd.sunk | while | flops 1006764032 | bytes 3932463 | solution.py:94
  400.7 3.5 dynamic_update_slice.37
  406.1 3.3 collective-permute-done.2
  413.1 6.7 %collective-permute-done.3 = f32[256,256]{1,0:T(8,128)S(1)} collective-permute-done((f32[256,256]{1,0:T(8,128)S(1)}, f32[256,256]{1,0:T(8,128)S(1)}, u32[]{:S(2)}, u32[]{:S(2)}) %collective-permute-start.3) | collective-permute-done | bytes 262176 | tf_op jit(solution)/shard_map/while/body/eval_jaxpr/ppermute | solution.py:25
  419.8 13.5 %conditional.8 = ((f32[512,1024]{1,0:T(8,128)}, f32[256,256]{1,0:T(8,128)S(1)})) conditional(s32[]{:T(128)} %convert_element_type.45, (f32[512,1024]{1,0:T(8,128)}, f32[256,256]{1,0:T(8,128)S(1)}) %tuple.172, (s32[]{:T(128)}, f32[512,1024]{1,0:T(8,128)}, f32[256,256]{1,0:T(8,128)S(1)}, s32[]{:T(128)}, pred[]{:T(512)}, ...), branch_computations={%region_1.1_spmd, %region_2.6_spmd} | conditional | flops 1006960640 | bytes 12321348 | solution.py:98
  423.2 6.6 %while.64 = (s32[]{:T(128)}, f32[768,256]{1,0:T(8,128)S(1)}, s32[]{:T(128)}, s32[]{:T(128)}, s32[]{:T(128)}, /*index=5*/f32[2,256,512]{2,1,0:T(8,128)S(1)}, f32[2,256,256]{2,1,0:T(8,128)S(1)}, s32[]{:T(128)}, s32[]{:T(128)}) while((s32[]{:T(128)}, f32[768,256]{1,0:T(8,128)S(1)}, s32[]{:T(128)}, s32[]{:T(128)}, s32[]{:T(128)}, ...), condition=%wide.region_6.5_spmd, body=%wide.region_3.4_spmd.sunk | while | flops 1006764032 | bytes 3932463 | solution.py:94
  429.8 3.5 dynamic_update_slice.35
  435.3 3.3 collective-permute-done
  442.3 6.5 %collective-permute-done.1 = f32[256,256]{1,0:T(8,128)S(1)} collective-permute-done((f32[256,256]{1,0:T(8,128)S(1)}, f32[256,256]{1,0:T(8,128)S(1)}, u32[]{:S(2)}, u32[]{:S(2)}) %collective-permute-start.1) | collective-permute-done | bytes 262176 | tf_op jit(solution)/shard_map/while/body/eval_jaxpr/ppermute | solution.py:25
  448.8 12.8 %conditional.9 = ((f32[512,1024]{1,0:T(8,128)}, f32[256,256]{1,0:T(8,128)S(1)})) conditional(s32[]{:T(128)} %convert_element_type.44, (f32[512,1024]{1,0:T(8,128)}, f32[256,256]{1,0:T(8,128)S(1)}) %tuple.174, (s32[]{:T(128)}, f32[512,1024]{1,0:T(8,128)}, f32[256,256]{1,0:T(8,128)S(1)}, s32[]{:T(128)}, pred[]{:T(512)}, ...), branch_computations={%region_7.7_spmd, %region_8.12_spmd} | conditional | flops 1006960640 | bytes 12321348 | solution.py:98
  452.1 6.6 %while.65 = (s32[]{:T(128)}, f32[768,256]{1,0:T(8,128)S(1)}, s32[]{:T(128)}, s32[]{:T(128)}, s32[]{:T(128)}, /*index=5*/f32[2,256,512]{2,1,0:T(8,128)S(1)}, f32[2,256,256]{2,1,0:T(8,128)S(1)}, s32[]{:T(128)}, s32[]{:T(128)}) while((s32[]{:T(128)}, f32[768,256]{1,0:T(8,128)S(1)}, s32[]{:T(128)}, s32[]{:T(128)}, s32[]{:T(128)}, ...), condition=%wide.region_12.11_spmd, body=%wide.region_9.10_spmd.sunk | while | flops 1006764032 | bytes 3932463 | solution.py:94
  463.6 3.3 collective-permute-done.2
  470.5 6.5 %collective-permute-done.3 = f32[256,256]{1,0:T(8,128)S(1)} collective-permute-done((f32[256,256]{1,0:T(8,128)S(1)}, f32[256,256]{1,0:T(8,128)S(1)}, u32[]{:S(2)}, u32[]{:S(2)}) %collective-permute-start.3) | collective-permute-done | bytes 262176 | tf_op jit(solution)/shard_map/while/body/eval_jaxpr/ppermute | solution.py:25
  479.0 8.2 %collective-permute-done = f32[256,256]{1,0:T(8,128)S(1)} collective-permute-done((f32[256,256]{1,0:T(8,128)S(1)}, f32[256,256]{1,0:T(8,128)S(1)}, u32[]{:S(2)}, u32[]{:S(2)}) %collective-permute-start) | collective-permute-done | bytes 262176 | tf_op jit(solution)/shard_map/while/body/eval_jaxpr/ppermute | solution.py:22
  491.1 8.0 %collective-permute-done.1 = f32[256,256]{1,0:T(8,128)S(1)} collective-permute-done((f32[256,256]{1,0:T(8,128)S(1)}, f32[256,256]{1,0:T(8,128)S(1)}, u32[]{:S(2)}, u32[]{:S(2)}) %collective-permute-start.1) | collective-permute-done | bytes 262176 | tf_op jit(solution)/shard_map/while/body/eval_jaxpr/ppermute | solution.py:25
  501.0 3.3 collective-permute-done.2
  508.0 6.5 %collective-permute-done.3 = f32[256,256]{1,0:T(8,128)S(1)} collective-permute-done((f32[256,256]{1,0:T(8,128)S(1)}, f32[256,256]{1,0:T(8,128)S(1)}, u32[]{:S(2)}, u32[]{:S(2)}) %collective-permute-start.3) | collective-permute-done | bytes 262176 | tf_op jit(solution)/shard_map/while/body/eval_jaxpr/ppermute | solution.py:25
  (183 shorter events, 179.8 us)
Async XLA Ops:
  6.5 3.2 copy-start
  6.5 70.6 %all-gather.2.cloned.1.call-start = ((), (), s32[]{:S(2)}) async-start(), calls=%async_computation.1 | async-start | bytes 2621440 | tf_op jit(solution)/shard_map/all_gather | solution.py:54
  11.3 65.9 %copy-start.1 = (s32[2,2]{1,0:T(2,128)S(1)}, s32[2,2]{1,0:T(2,128)}, u32[]{:S(2)}) copy-start(s32[2,2]{1,0:T(2,128)} %param.21) | copy-start | bytes 52
  11.3 52.9 %all-to-all-start = ((f32[2,2,256,256]{3,1,0,2:T(2,128)}), f32[2,2,256,256]{3,1,0,2:T(2,128)S(1)}, u32[]{:S(2)}, u32[]{:S(2)}) async-start(f32[2,2,256,256]{3,1,0,2:T(2,128)} %bitcast.12), calls=%async_computation | async-start | bytes 2097152 | tf_op jit(solution)/shard_map/all_to_all | solution.py:12
  77.3 6.8 %collective-permute-start = (f32[256,256]{1,0:T(8,128)S(1)}, f32[256,256]{1,0:T(8,128)S(1)}, u32[]{:S(2)}, u32[]{:S(2)}) collective-permute-start(f32[256,256]{1,0:T(8,128)S(1)} %get-tuple-element.1140), channel_id=1, source_target_pairs={{0,4},{4,8},{8,12},{12,16},{16,20},{20,24},{24,28},{1,5},{5,9},{9,... | collective-permute-start | bytes 786440 | tf_op jit(solution)/shard_map/while/body/eval_jaxpr/ppermute | solution.py:22
  85.8 8.4 %collective-permute-start.1 = (f32[256,256]{1,0:T(8,128)S(1)}, f32[256,256]{1,0:T(8,128)S(1)}, u32[]{:S(2)}, u32[]{:S(2)}) collective-permute-start(f32[256,256]{1,0:T(8,128)S(1)} %get-tuple-element.1142), channel_id=1, source_target_pairs={{4,0},{8,4},{12,8},{16,12},{20,16},{24,20},{28,24},{5,1},{9,5},{13... | collective-permute-start | bytes 786440 | tf_op jit(solution)/shard_map/while/body/eval_jaxpr/ppermute | solution.py:25
  94.3 5.2 collective-permute-start.2
  101.3 8.4 %collective-permute-start.3 = (f32[256,256]{1,0:T(8,128)S(1)}, f32[256,256]{1,0:T(8,128)S(1)}, u32[]{:S(2)}, u32[]{:S(2)}) collective-permute-start(f32[256,256]{1,0:T(8,128)S(1)} %get-tuple-element.1146), channel_id=1, source_target_pairs={{4,0},{8,4},{12,8},{16,12},{20,16},{24,20},{28,24},{5,1},{9,5},{13... | collective-permute-start | bytes 786440 | tf_op jit(solution)/shard_map/while/body/eval_jaxpr/ppermute | solution.py:25
  109.7 5.2 collective-permute-start
  116.7 9.5 %collective-permute-start.1 = (f32[256,256]{1,0:T(8,128)S(1)}, f32[256,256]{1,0:T(8,128)S(1)}, u32[]{:S(2)}, u32[]{:S(2)}) collective-permute-start(f32[256,256]{1,0:T(8,128)S(1)} %get-tuple-element.1142), channel_id=1, source_target_pairs={{4,0},{8,4},{12,8},{16,12},{20,16},{24,20},{28,24},{5,1},{9,5},{13... | collective-permute-start | bytes 786440 | tf_op jit(solution)/shard_map/while/body/eval_jaxpr/ppermute | solution.py:25
  126.2 16.6 %collective-permute-start.2 = (f32[256,256]{1,0:T(8,128)S(1)}, f32[256,256]{1,0:T(8,128)S(1)}, u32[]{:S(2)}, u32[]{:S(2)}) collective-permute-start(f32[256,256]{1,0:T(8,128)S(1)} %get-tuple-element.1144), channel_id=1, source_target_pairs={{0,4},{4,8},{8,12},{12,16},{16,20},{20,24},{24,28},{1,5},{5,9},{9,... | collective-permute-start | bytes 786440 | tf_op jit(solution)/shard_map/while/body/eval_jaxpr/ppermute | solution.py:22
  144.5 23.7 %collective-permute-start.3 = (f32[256,256]{1,0:T(8,128)S(1)}, f32[256,256]{1,0:T(8,128)S(1)}, u32[]{:S(2)}, u32[]{:S(2)}) collective-permute-start(f32[256,256]{1,0:T(8,128)S(1)} %get-tuple-element.1146), channel_id=1, source_target_pairs={{4,0},{8,4},{12,8},{16,12},{20,16},{24,20},{28,24},{5,1},{9,5},{13... | collective-permute-start | bytes 786440 | tf_op jit(solution)/shard_map/while/body/eval_jaxpr/ppermute | solution.py:25
  168.3 17.7 %collective-permute-start = (f32[256,256]{1,0:T(8,128)S(1)}, f32[256,256]{1,0:T(8,128)S(1)}, u32[]{:S(2)}, u32[]{:S(2)}) collective-permute-start(f32[256,256]{1,0:T(8,128)S(1)} %get-tuple-element.1140), channel_id=1, source_target_pairs={{0,4},{4,8},{8,12},{12,16},{16,20},{20,24},{24,28},{1,5},{5,9},{9,... | collective-permute-start | bytes 786440 | tf_op jit(solution)/shard_map/while/body/eval_jaxpr/ppermute | solution.py:22
  187.8 23.8 %collective-permute-start.1 = (f32[256,256]{1,0:T(8,128)S(1)}, f32[256,256]{1,0:T(8,128)S(1)}, u32[]{:S(2)}, u32[]{:S(2)}) collective-permute-start(f32[256,256]{1,0:T(8,128)S(1)} %get-tuple-element.1142), channel_id=1, source_target_pairs={{4,0},{8,4},{12,8},{16,12},{20,16},{24,20},{28,24},{5,1},{9,5},{13... | collective-permute-start | bytes 786440 | tf_op jit(solution)/shard_map/while/body/eval_jaxpr/ppermute | solution.py:25
  211.5 18.6 %collective-permute-start.2 = (f32[256,256]{1,0:T(8,128)S(1)}, f32[256,256]{1,0:T(8,128)S(1)}, u32[]{:S(2)}, u32[]{:S(2)}) collective-permute-start(f32[256,256]{1,0:T(8,128)S(1)} %get-tuple-element.1144), channel_id=1, source_target_pairs={{0,4},{4,8},{8,12},{12,16},{16,20},{20,24},{24,28},{1,5},{5,9},{9,... | collective-permute-start | bytes 786440 | tf_op jit(solution)/shard_map/while/body/eval_jaxpr/ppermute | solution.py:22
  231.9 9.5 %collective-permute-start.3 = (f32[256,256]{1,0:T(8,128)S(1)}, f32[256,256]{1,0:T(8,128)S(1)}, u32[]{:S(2)}, u32[]{:S(2)}) collective-permute-start(f32[256,256]{1,0:T(8,128)S(1)} %get-tuple-element.1146), channel_id=1, source_target_pairs={{4,0},{8,4},{12,8},{16,12},{20,16},{24,20},{28,24},{5,1},{9,5},{13... | collective-permute-start | bytes 786440 | tf_op jit(solution)/shard_map/while/body/eval_jaxpr/ppermute | solution.py:25
  254.9 5.2 %collective-permute-start = (f32[256,256]{1,0:T(8,128)S(1)}, f32[256,256]{1,0:T(8,128)S(1)}, u32[]{:S(2)}, u32[]{:S(2)}) collective-permute-start(f32[256,256]{1,0:T(8,128)S(1)} %get-tuple-element.1140), channel_id=1, source_target_pairs={{0,4},{4,8},{8,12},{12,16},{16,20},{20,24},{24,28},{1,5},{5,9},{9,... | collective-permute-start | bytes 786440 | tf_op jit(solution)/shard_map/while/body/eval_jaxpr/ppermute | solution.py:22
  262.0 9.3 %collective-permute-start.1 = (f32[256,256]{1,0:T(8,128)S(1)}, f32[256,256]{1,0:T(8,128)S(1)}, u32[]{:S(2)}, u32[]{:S(2)}) collective-permute-start(f32[256,256]{1,0:T(8,128)S(1)} %get-tuple-element.1142), channel_id=1, source_target_pairs={{4,0},{8,4},{12,8},{16,12},{20,16},{24,20},{28,24},{5,1},{9,5},{13... | collective-permute-start | bytes 786440 | tf_op jit(solution)/shard_map/while/body/eval_jaxpr/ppermute | solution.py:25
  284.8 5.2 %collective-permute-start.2 = (f32[256,256]{1,0:T(8,128)S(1)}, f32[256,256]{1,0:T(8,128)S(1)}, u32[]{:S(2)}, u32[]{:S(2)}) collective-permute-start(f32[256,256]{1,0:T(8,128)S(1)} %get-tuple-element.1144), channel_id=1, source_target_pairs={{0,4},{4,8},{8,12},{12,16},{16,20},{20,24},{24,28},{1,5},{5,9},{9,... | collective-permute-start | bytes 786440 | tf_op jit(solution)/shard_map/while/body/eval_jaxpr/ppermute | solution.py:22
  291.8 8.6 %collective-permute-start.3 = (f32[256,256]{1,0:T(8,128)S(1)}, f32[256,256]{1,0:T(8,128)S(1)}, u32[]{:S(2)}, u32[]{:S(2)}) collective-permute-start(f32[256,256]{1,0:T(8,128)S(1)} %get-tuple-element.1146), channel_id=1, source_target_pairs={{4,0},{8,4},{12,8},{16,12},{20,16},{24,20},{28,24},{5,1},{9,5},{13... | collective-permute-start | bytes 786440 | tf_op jit(solution)/shard_map/while/body/eval_jaxpr/ppermute | solution.py:25
  314.0 5.2 %collective-permute-start = (f32[256,256]{1,0:T(8,128)S(1)}, f32[256,256]{1,0:T(8,128)S(1)}, u32[]{:S(2)}, u32[]{:S(2)}) collective-permute-start(f32[256,256]{1,0:T(8,128)S(1)} %get-tuple-element.1140), channel_id=1, source_target_pairs={{0,4},{4,8},{8,12},{12,16},{16,20},{20,24},{24,28},{1,5},{5,9},{9,... | collective-permute-start | bytes 786440 | tf_op jit(solution)/shard_map/while/body/eval_jaxpr/ppermute | solution.py:22
  321.0 9.8 %collective-permute-start.1 = (f32[256,256]{1,0:T(8,128)S(1)}, f32[256,256]{1,0:T(8,128)S(1)}, u32[]{:S(2)}, u32[]{:S(2)}) collective-permute-start(f32[256,256]{1,0:T(8,128)S(1)} %get-tuple-element.1142), channel_id=1, source_target_pairs={{4,0},{8,4},{12,8},{16,12},{20,16},{24,20},{28,24},{5,1},{9,5},{13... | collective-permute-start | bytes 786440 | tf_op jit(solution)/shard_map/while/body/eval_jaxpr/ppermute | solution.py:25
  343.7 5.8 %collective-permute-start.2 = (f32[256,256]{1,0:T(8,128)S(1)}, f32[256,256]{1,0:T(8,128)S(1)}, u32[]{:S(2)}, u32[]{:S(2)}) collective-permute-start(f32[256,256]{1,0:T(8,128)S(1)} %get-tuple-element.1144), channel_id=1, source_target_pairs={{0,4},{4,8},{8,12},{12,16},{16,20},{20,24},{24,28},{1,5},{5,9},{9,... | collective-permute-start | bytes 786440 | tf_op jit(solution)/shard_map/while/body/eval_jaxpr/ppermute | solution.py:22
  351.2 9.5 %collective-permute-start.3 = (f32[256,256]{1,0:T(8,128)S(1)}, f32[256,256]{1,0:T(8,128)S(1)}, u32[]{:S(2)}, u32[]{:S(2)}) collective-permute-start(f32[256,256]{1,0:T(8,128)S(1)} %get-tuple-element.1146), channel_id=1, source_target_pairs={{4,0},{8,4},{12,8},{16,12},{20,16},{24,20},{28,24},{5,1},{9,5},{13... | collective-permute-start | bytes 786440 | tf_op jit(solution)/shard_map/while/body/eval_jaxpr/ppermute | solution.py:25
  374.3 5.2 %collective-permute-start = (f32[256,256]{1,0:T(8,128)S(1)}, f32[256,256]{1,0:T(8,128)S(1)}, u32[]{:S(2)}, u32[]{:S(2)}) collective-permute-start(f32[256,256]{1,0:T(8,128)S(1)} %get-tuple-element.1140), channel_id=1, source_target_pairs={{0,4},{4,8},{8,12},{12,16},{16,20},{20,24},{24,28},{1,5},{5,9},{9,... | collective-permute-start | bytes 786440 | tf_op jit(solution)/shard_map/while/body/eval_jaxpr/ppermute | solution.py:22
  381.3 9.3 %collective-permute-start.1 = (f32[256,256]{1,0:T(8,128)S(1)}, f32[256,256]{1,0:T(8,128)S(1)}, u32[]{:S(2)}, u32[]{:S(2)}) collective-permute-start(f32[256,256]{1,0:T(8,128)S(1)} %get-tuple-element.1142), channel_id=1, source_target_pairs={{4,0},{8,4},{12,8},{16,12},{20,16},{24,20},{28,24},{5,1},{9,5},{13... | collective-permute-start | bytes 786440 | tf_op jit(solution)/shard_map/while/body/eval_jaxpr/ppermute | solution.py:25
  404.2 5.2 %collective-permute-start.2 = (f32[256,256]{1,0:T(8,128)S(1)}, f32[256,256]{1,0:T(8,128)S(1)}, u32[]{:S(2)}, u32[]{:S(2)}) collective-permute-start(f32[256,256]{1,0:T(8,128)S(1)} %get-tuple-element.1144), channel_id=1, source_target_pairs={{0,4},{4,8},{8,12},{12,16},{16,20},{20,24},{24,28},{1,5},{5,9},{9,... | collective-permute-start | bytes 786440 | tf_op jit(solution)/shard_map/while/body/eval_jaxpr/ppermute | solution.py:22
  411.2 8.6 %collective-permute-start.3 = (f32[256,256]{1,0:T(8,128)S(1)}, f32[256,256]{1,0:T(8,128)S(1)}, u32[]{:S(2)}, u32[]{:S(2)}) collective-permute-start(f32[256,256]{1,0:T(8,128)S(1)} %get-tuple-element.1146), channel_id=1, source_target_pairs={{4,0},{8,4},{12,8},{16,12},{20,16},{24,20},{28,24},{5,1},{9,5},{13... | collective-permute-start | bytes 786440 | tf_op jit(solution)/shard_map/while/body/eval_jaxpr/ppermute | solution.py:25
  433.3 5.2 %collective-permute-start = (f32[256,256]{1,0:T(8,128)S(1)}, f32[256,256]{1,0:T(8,128)S(1)}, u32[]{:S(2)}, u32[]{:S(2)}) collective-permute-start(f32[256,256]{1,0:T(8,128)S(1)} %get-tuple-element.1140), channel_id=1, source_target_pairs={{0,4},{4,8},{8,12},{12,16},{16,20},{20,24},{24,28},{1,5},{5,9},{9,... | collective-permute-start | bytes 786440 | tf_op jit(solution)/shard_map/while/body/eval_jaxpr/ppermute | solution.py:22
  440.3 8.4 %collective-permute-start.1 = (f32[256,256]{1,0:T(8,128)S(1)}, f32[256,256]{1,0:T(8,128)S(1)}, u32[]{:S(2)}, u32[]{:S(2)}) collective-permute-start(f32[256,256]{1,0:T(8,128)S(1)} %get-tuple-element.1142), channel_id=1, source_target_pairs={{4,0},{8,4},{12,8},{16,12},{20,16},{24,20},{28,24},{5,1},{9,5},{13... | collective-permute-start | bytes 786440 | tf_op jit(solution)/shard_map/while/body/eval_jaxpr/ppermute | solution.py:25
  461.6 5.2 %collective-permute-start.2 = (f32[256,256]{1,0:T(8,128)S(1)}, f32[256,256]{1,0:T(8,128)S(1)}, u32[]{:S(2)}, u32[]{:S(2)}) collective-permute-start(f32[256,256]{1,0:T(8,128)S(1)} %get-tuple-element.1144), channel_id=1, source_target_pairs={{0,4},{4,8},{8,12},{12,16},{16,20},{20,24},{24,28},{1,5},{5,9},{9,... | collective-permute-start | bytes 786440 | tf_op jit(solution)/shard_map/while/body/eval_jaxpr/ppermute | solution.py:22
  468.6 8.4 %collective-permute-start.3 = (f32[256,256]{1,0:T(8,128)S(1)}, f32[256,256]{1,0:T(8,128)S(1)}, u32[]{:S(2)}, u32[]{:S(2)}) collective-permute-start(f32[256,256]{1,0:T(8,128)S(1)} %get-tuple-element.1146), channel_id=1, source_target_pairs={{4,0},{8,4},{12,8},{16,12},{20,16},{24,20},{28,24},{5,1},{9,5},{13... | collective-permute-start | bytes 786440 | tf_op jit(solution)/shard_map/while/body/eval_jaxpr/ppermute | solution.py:25
  477.1 10.2 %collective-permute-start = (f32[256,256]{1,0:T(8,128)S(1)}, f32[256,256]{1,0:T(8,128)S(1)}, u32[]{:S(2)}, u32[]{:S(2)}) collective-permute-start(f32[256,256]{1,0:T(8,128)S(1)} %get-tuple-element.1140), channel_id=1, source_target_pairs={{0,4},{4,8},{8,12},{12,16},{16,20},{20,24},{24,28},{1,5},{5,9},{9,... | collective-permute-start | bytes 786440 | tf_op jit(solution)/shard_map/while/body/eval_jaxpr/ppermute | solution.py:22
  489.0 10.1 %collective-permute-start.1 = (f32[256,256]{1,0:T(8,128)S(1)}, f32[256,256]{1,0:T(8,128)S(1)}, u32[]{:S(2)}, u32[]{:S(2)}) collective-permute-start(f32[256,256]{1,0:T(8,128)S(1)} %get-tuple-element.1142), channel_id=1, source_target_pairs={{4,0},{8,4},{12,8},{16,12},{20,16},{24,20},{28,24},{5,1},{9,5},{13... | collective-permute-start | bytes 786440 | tf_op jit(solution)/shard_map/while/body/eval_jaxpr/ppermute | solution.py:25
  499.0 5.2 collective-permute-start.2
  506.0 8.4 %collective-permute-start.3 = (f32[256,256]{1,0:T(8,128)S(1)}, f32[256,256]{1,0:T(8,128)S(1)}, u32[]{:S(2)}, u32[]{:S(2)}) collective-permute-start(f32[256,256]{1,0:T(8,128)S(1)} %get-tuple-element.1146), channel_id=1, source_target_pairs={{4,0},{8,4},{12,8},{16,12},{20,16},{24,20},{28,24},{5,1},{9,5},{13... | collective-permute-start | bytes 786440 | tf_op jit(solution)/shard_map/while/body/eval_jaxpr/ppermute | solution.py:25
Sparse Core Ops, SparseCore 0:
  9.9 67.2 all-gather.1
